TPU v7x, 32 devices: a whole 2x2x4 slice. The times are simulated.
32 devices in a mesh: dp: 8 (over y, x, core), expert: 4 (over z).
Axes of the slice: x: 2, y: 2, z: 4, core: 2. Of those that a mesh axis runs over, the one named last changes fastest.
Arguments:
- grad_out: bfloat16 [2048, 2048], P('dp', 'expert'), may hold values from -48 to 48
- saved_inputs: bfloat16 [2048, 2048], P('dp', 'expert'), may hold values from -6 to 6
- router_probs: float32 [4, 2048], P('expert', 'dp'), may hold values from 0 to 1, as said below
- chosen: int32 [4, 512], replicated, may hold values from 0 to 2047, as said below
- gate_pre: bfloat16 [4, 512, 7168], P('expert', None, 'dp'), may hold values from -6 to 6
- up_pre: bfloat16 [4, 512, 7168], P('expert', None, 'dp'), may hold values from -6 to 6
- w_down: bfloat16 [4, 7168, 2048], P('expert', 'dp'), may hold values from -0.0625 to 0.0625
- w_up: bfloat16 [4, 7168, 2048], P('expert', 'dp'), may hold values from -0.125 to 0.125
Outputs:
- grad_tokens: bfloat16 [2048, 2048], P('dp', 'expert')
- grad_logits: float32 [4, 2048], P('expert', 'dp')
- grad_down: bfloat16 [4, 7168, 2048], P('expert', 'dp')
- grad_up: bfloat16 [4, 7168, 2048], P('expert', 'dp')
- grad_gate_pre: bfloat16 [4, 512, 7168], P('expert', None, 'dp')
Inputs may be any that keep to these rules, and one draw needn't show every extreme that they name: `chosen`: every row lists 512 different tokens in increasing order. Among the 256 consecutive tokens of one index of dp, an expert chooses at most 96, and every expert chooses exactly 96 from some index of dp. `router_probs`: each token's probabilities over the 4 experts are positive and sum to one.
All inputs are finite; a program needn't handle non-finite values.
Results may differ from a plain program's by a relative error of at most 0.04.
Values may be sent and summed in bfloat16 or wider, within the bound.
A program may use at most 64 MiB of HBM per device.

v0:
```python
import jax
import jax.numpy as jnp
from jax import lax
from jax.sharding import PartitionSpec as P


def shard_slots(chosen, shard_index, capacity, tok_dev):
    owners = chosen // tok_dev
    firsts = jnp.sum((owners < shard_index).astype(jnp.int32), axis=1)
    counts = jnp.sum((owners == shard_index).astype(jnp.int32), axis=1)
    offsets = jnp.arange(capacity, dtype=jnp.int32)
    places = jnp.clip(firsts[:, None] + offsets[None, :], 0, chosen.shape[1] - 1)
    picked = jnp.take_along_axis(chosen, places, axis=1)
    return jnp.where(offsets[None, :] < counts[:, None], picked - shard_index * tok_dev, -1)


def grad_block(dout_rows, gate_rows, gate_piece, up_piece, down_block):
    gate_value = gate_piece.astype(jnp.float32)
    up_value = up_piece.astype(jnp.float32)
    sigmoid_gate = jax.nn.sigmoid(gate_value)
    active = gate_value * sigmoid_gate
    hidden = active * up_value
    raw_grad = lax.dot_general(
        dout_rows, down_block, (((1,), (1,)), ((), ())), preferred_element_type=jnp.float32
    )
    dot_sums = jnp.sum(hidden * raw_grad, axis=1)
    hid_grad = gate_rows.astype(jnp.float32)[:, None] * raw_grad
    up_grad = (hid_grad * active).astype(jnp.bfloat16)
    gate_grad = (
        hid_grad * up_value * sigmoid_gate * (1.0 + gate_value * (1.0 - sigmoid_gate))
    ).astype(jnp.bfloat16)
    out_grad = gate_rows[:, None] * dout_rows
    down_term = lax.dot_general(
        hidden.astype(jnp.bfloat16),
        out_grad,
        (((0,), (0,)), ((), ())),
        preferred_element_type=jnp.float32,
    )
    return (down_term, up_grad, gate_grad, dot_sums)


def local(grad_out, saved_inputs, router_probs, chosen, gate_pre, up_pre, w_down, w_up):
    tok_dev = grad_out.shape[0]
    width_dev = grad_out.shape[1]
    shard_count = lax.axis_size("dp")
    shard_index = lax.axis_index("dp")
    expert = lax.axis_index("expert")
    experts_all, slot_total = chosen.shape
    capacity = 3 * slot_total // (2 * shard_count)
    local_rows = shard_slots(chosen, shard_index, capacity, tok_dev)
    token_iota = jnp.arange(tok_dev, dtype=jnp.int32)
    picker = local_rows.reshape(-1)[:, None] == token_iota[None, :]
    stacked = jnp.concatenate([grad_out, saved_inputs], axis=1)
    packed = jnp.dot(
        picker.astype(jnp.bfloat16), stacked, preferred_element_type=jnp.float32
    ).astype(jnp.bfloat16)
    packed = packed.reshape(experts_all, capacity, 2 * width_dev)
    sent_grad = packed[:, :, :width_dev]
    sent_input = packed[:, :, width_dev:]
    dout_rows, input_rows = (
        lax.all_to_all(sent_grad, "expert", split_axis=0, concat_axis=2, tiled=True),
        lax.all_to_all(sent_input, "expert", split_axis=0, concat_axis=2, tiled=True),
    )
    own_rows = lax.dynamic_index_in_dim(local_rows, expert, 0, keepdims=False)
    router_gate = router_probs[0]
    own_hit = own_rows[:, None] == token_iota[None, :]
    gate_slot = jnp.sum(jnp.where(own_hit, router_gate[None, :], 0.0), axis=1).astype(jnp.bfloat16)
    chosen_row = lax.dynamic_index_in_dim(chosen, expert, 0, keepdims=False)
    row_owners = chosen_row // tok_dev
    shard_ids = jnp.arange(shard_count, dtype=jnp.int32)
    firsts = jnp.sum((row_owners[None, :] < shard_ids[:, None]).astype(jnp.int32), axis=1)
    counts = jnp.sum((row_owners[None, :] == shard_ids[:, None]).astype(jnp.int32), axis=1)
    rows_all = shard_count * capacity
    padded_ids = jnp.arange(rows_all, dtype=jnp.int32)
    source = padded_ids // capacity
    within = padded_ids % capacity
    is_valid = within < counts[source]
    compact = jnp.clip(firsts[source] + within, 0, slot_total - 1)
    gate_rows_all = jnp.where(is_valid[:, None], gate_pre[0][compact], jnp.zeros((), jnp.bfloat16))
    up_rows_all = jnp.where(is_valid[:, None], up_pre[0][compact], jnp.zeros((), jnp.bfloat16))
    down_block = w_down[0]
    upw_block = w_up[0]
    piece_grad = lax.all_gather(dout_rows[0], "dp", axis=0, tiled=True)
    piece_gate = lax.all_gather(gate_slot, "dp", axis=0, tiled=True)
    up_piece = up_rows_all
    down_term, up_grad, gate_grad, dot_sums = grad_block(
        piece_grad, piece_gate, gate_rows_all, up_piece, down_block
    )
    up_piece = up_grad
    up_sum = lax.dot_general(
        up_piece,
        lax.all_gather(input_rows[0], "dp", axis=0, tiled=True),
        (((0,), (0,)), ((), ())),
        preferred_element_type=jnp.float32,
    )
    dx_part = jnp.dot(up_grad, upw_block, preferred_element_type=jnp.float32)
    dx_back, dots_back = (
        lax.psum_scatter(
            dx_part.astype(jnp.bfloat16), "dp", scatter_dimension=0, tiled=True
        ).astype(jnp.float32),
        lax.psum_scatter(
            dot_sums.astype(jnp.bfloat16), "dp", scatter_dimension=0, tiled=True
        ).astype(jnp.float32),
    )
    spread = lax.all_to_all(
        dx_back[None].astype(jnp.bfloat16), "expert", split_axis=2, concat_axis=0, tiled=True
    ).astype(jnp.float32)
    placer = picker.astype(jnp.float32)
    grad_tokens = lax.dot_general(
        placer,
        spread.reshape(experts_all * capacity, -1),
        (((0,), (0,)), ((), ())),
        precision=lax.Precision.HIGHEST,
        preferred_element_type=jnp.float32,
    ).astype(jnp.bfloat16)
    gate_tokens = jnp.sum(jnp.where(own_hit, dots_back[:, None], 0.0), axis=0)
    weighted = lax.psum(router_gate * gate_tokens, "expert")
    grad_logits = (router_gate * (gate_tokens - weighted))[None, :]
    slot_iota = jnp.arange(slot_total, dtype=jnp.int32)
    slot_place = row_owners * capacity + slot_iota - firsts[row_owners]
    grad_gate_pre = gate_grad[slot_place][None]
    return (
        grad_tokens,
        grad_logits,
        down_term.astype(jnp.bfloat16)[None],
        up_sum.astype(jnp.bfloat16)[None],
        grad_gate_pre,
    )


def solution(mesh):
    in_specs = (
        P("dp", "expert"),
        P("dp", "expert"),
        P("expert", "dp"),
        P(),
        P("expert", None, "dp"),
        P("expert", None, "dp"),
        P("expert", "dp", None),
        P("expert", "dp", None),
    )
    out_specs = (
        P("dp", "expert"),
        P("expert", "dp"),
        P("expert", "dp", None),
        P("expert", "dp", None),
        P("expert", None, "dp"),
    )
    return jax.shard_map(local, mesh=mesh, in_specs=in_specs, out_specs=out_specs, check_vma=False)
```

profile of v0, /device:TPU:0, one launch (start us, length us, event | category | flops | bytes accessed | tf_op | source)
XLA Modules:
  0.0 205.5 jit_solution(15687441909129225498)
XLA Ops:
  7.2 0.9 convert_reduce_fusion.2
  8.2 0.1 lt.132
  8.4 0.1 reshape.392
  8.5 4.9 %gather_fusion.3 = s32[384]{0:T(512)S(1)} fusion(s32[4,512]{1,0:T(4,128)} %param.11, s32[384]{0:T(512)S(1)} %reshape.392), kind=kCustom, calls=%fused_computation.3 | custom fusion | bytes 6144 | tf_op jit(solution)/shard_map/jit(take_along_axis)/gather | solution.py:13
  13.5 0.1 add.188
  13.6 0.1 lt.135
  13.7 1.4 convolution_convert_fusion
  15.2 17.8 %all_to_all.45 = bf16[4,96,512]{2,1,0:T(8,128)(2,1)S(1)} all-to-all(bf16[4,96,512]{2,1,0:T(8,128)(2,1)S(1)} %get-tuple-element.14), channel_id=1, replica_groups=mesh['dp'=8,'expert'=4] {'expert'}, dimensions={0} | all-to-all | bytes 786432 | tf_op jit(solution)/shard_map/all_to_all | solution.py:61
  33.1 0.3 copy.24
  33.4 0.8 copy.29
  34.3 13.8 %all_to_all.46 = bf16[4,96,512]{2,1,0:T(8,128)(2,1)S(1)} all-to-all(bf16[4,96,512]{2,1,0:T(8,128)(2,1)S(1)} %get-tuple-element.13), channel_id=1, replica_groups=mesh['dp'=8,'expert'=4] {'expert'}, dimensions={0} | all-to-all | bytes 786432 | tf_op jit(solution)/shard_map/all_to_all | solution.py:62
  48.0 0.3 copy.28
  48.4 0.8 copy.30
  49.3 0.1 reshape.395
  49.4 0.1 convert_reduce_fusion.1
  49.6 0.7 fusion.39
  50.3 4.4 %fusion.30 = s32[768]{0:T(1024)S(1)} fusion(s32[]{:T(128)} %bitcast.18, s32[]{:T(128)} %bitcast.19, s32[]{:T(128)} %bitcast.20, s32[]{:T(128)} %bitcast.21, s32[]{:T(128)} %bitcast.22, s32[]{:T(128)} %bitcast.24, s32[]{:T(128)} %bitcast.23), kind=kLoop, calls=%fused_computation.102 | loop fusion | flops 17664 | bytes 3100 | tf_op jit(solution)/shard_map/gather | solution.py:78
  54.6 0.6 broadcast_select_fusion.2
  55.4 2.8 %gather_fusion = bf16[768,896]{1,0:T(8,128)(2,1)S(1)} fusion(bf16[512,896]{1,0:T(8,128)(2,1)S(1)} %bitcast.77, s32[1024]{0:T(1024)S(1)} %pad_clamp_fusion.1), kind=kCustom, calls=%fused_computation | custom fusion | bytes 2755584 | tf_op jit(solution)/shard_map/gather | solution.py:79
  58.2 3.5 %gather_fusion.1 = bf16[768,896]{1,0:T(8,128)(2,1)} fusion(bf16[512,896]{1,0:T(8,128)(2,1)S(1)} %bitcast.78, s32[1024]{0:T(1024)S(1)} %pad_clamp_fusion.1), kind=kCustom, calls=%fused_computation.1 | custom fusion | bytes 2755584 | tf_op jit(solution)/shard_map/gather | solution.py:80
  61.7 0.7 fusion.38
  63.7 4.5 %fusion.31 = s32[768]{0:T(1024)S(1)} fusion(s32[]{:T(128)} %bitcast.9, s32[]{:T(128)} %bitcast.10, s32[]{:T(128)} %bitcast.11, s32[]{:T(128)} %bitcast.12, s32[]{:T(128)} %bitcast.13, s32[]{:T(128)} %bitcast.15, s32[]{:T(128)} %bitcast.14), kind=kLoop, calls=%fused_computation.103 | loop fusion | flops 17664 | bytes 3100 | tf_op jit(solution)/shard_map/gather | solution.py:77
  68.3 0.1 subtract_select_fusion
  68.3 0.7 fusion.25
  69.0 8.6 %multiply_reduce_fusion = (bf16[768]{0:T(1024)(128)(2,1)S(1)}, f32[768,896]{1,0:T(8,128)}) fusion(bf16[768,896]{1,0:T(8,128)(2,1)} %gather_fusion.1, pred[768]{0:T(1024)(128)(4,1)S(1)} %fusion.25, bf16[768,896]{1,0:T(8,128)(2,1)S(1)} %gather_fusion, bf16[768,2048]{1,0:T(8,128)(2,1)} %all-gather.3.cloned.1.call-done, bf16[1,896,2048]{2,1,0:T(8,128)(2,1)} %param.14), kind=kOutput, calls=%fused_computation.24 | convolution fusion | flops 2826140928 | bytes 12323072 | tf_op jit(solution)/shard_map/dot_general | solution.py:23
  77.6 12.2 %all-reduce.1 = bf16[768]{0:T(1024)(128)(2,1)S(1)} all-reduce(bf16[768]{0:T(1024)(128)(2,1)S(1)} %get-tuple-element.33), channel_id=3, replica_groups=mesh['dp'=8,'expert'=4] {'dp'}, use_global_device_ids=true, to_apply=%region_7.8.clone | all-reduce | flops 768 | bytes 3072
  89.9 0.2 select_reduce_fusion
  90.1 0.2 dynamic-update-slice
  90.4 12.3 %all-reduce = bf16[768]{0:T(1024)(128)(2,1)S(1)} all-reduce(bf16[768]{0:T(1024)(128)(2,1)S(1)} %dynamic-update-slice), channel_id=1, replica_groups=mesh['dp'=8,'expert'=4] {'dp'}, use_global_device_ids=true, to_apply=%add | all-reduce | flops 768 | bytes 3072
  102.7 8.7 %fusion.4 = bf16[768,2048]{1,0:T(8,128)(2,1)} fusion(bf16[1,896,2048]{2,1,0:T(8,128)(2,1)} %param.15, f32[768,896]{1,0:T(8,128)} %get-tuple-element.34, f32[768]{0:T(1024)S(1)} %convert_element_type.65, bf16[768,896]{1,0:T(8,128)(2,1)S(1)} %gather_fusion, pred[768]{0:T(1024)(128)(4,1)S(1)} %fusion.25), kind=kOutput, calls=%fused_computation.15 | convolution fusion | flops 2826338304 | bytes 10948352 | tf_op jit(solution)/shard_map/dot_general | solution.py:96
  111.5 4.4 %compare_select_fusion.4 = (s32[512,1]{0,1:T(1,128)S(1)}, s32[512,1]{0,1:T(1,128)S(1)}) fusion(s32[]{:T(128)} %bitcast.18, s32[]{:T(128)} %bitcast.19, s32[]{:T(128)} %bitcast.20, s32[]{:T(128)} %bitcast.21, s32[]{:T(128)} %bitcast.22, s32[]{:T(128)} %bitcast.24, s32[]{:T(128)} %bitcast.23, s32[4,512]{1,0:T(4,128)S(1)} %copy-done.1, s32[]{:T(128)S(6)} %select_n.171), kind=kLoop, calls=%fused_computation.62 | loop fusion | flops 15360 | bytes 6176 | tf_op jit(solution)/shard_map/gather | solution.py:120
  115.9 0.6 broadcast_select_fusion.3
  116.6 8.7 %convert_bitcast_fusion = bf16[1,896,2048]{2,1,0:T(8,128)(2,1)} fusion(bf16[768,2048]{1,0:T(8,128)(2,1)} %all-gather.5.cloned.1.call-done, f32[768,896]{1,0:T(8,128)} %get-tuple-element.34, f32[768]{0:T(1024)S(1)} %convert_element_type.65, bf16[768,896]{1,0:T(8,128)(2,1)S(1)} %gather_fusion, pred[768]{0:T(1024)(128)(4,1)S(1)} %fusion.25), kind=kOutput, calls=%fused_computation.11 | convolution fusion | flops 2826600448 | bytes 10948352 | tf_op jit(solution)/shard_map/dot_general | solution.py:90
  125.3 5.6 %convert_bitcast_fusion.1 = bf16[1,896,2048]{2,1,0:T(8,128)(2,1)} fusion(bf16[768,2048]{1,0:T(8,128)(2,1)S(1)} %copy-done.7, bf16[768]{0:T(1024)(128)(2,1)S(1)} %all-reduce, bf16[768,896]{1,0:T(8,128)(2,1)S(1)} %copy-done.4, pred[768]{0:T(1024)(128)(4,1)S(1)} %fusion.25, bf16[768,896]{1,0:T(8,128)(2,1)S(1)} %gather_fusion), kind=kOutput, calls=%fused_computation.12 | convolution fusion | flops 2828861440 | bytes 9570560 | tf_op jit(solution)/shard_map/dot_general | solution.py:33
  130.9 25.4 %reduce-scatter.2.cloned.1.call-done = bf16[96,2048]{1,0:T(8,128)(2,1)} async-done(((bf16[768,2048]{1,0:T(8,128)(2,1)}), bf16[96,2048]{1,0:T(8,128)(2,1)}) %reduce-scatter.2.cloned.1.call-update) | async-done | bytes 393232 | tf_op jit(solution)/shard_map/reduce_scatter | solution.py:98
  156.3 2.3 %copy.25 = bf16[1,96,2048]{1,0,2:T(2,128)(2,1)S(1)} copy(bf16[1,96,2048]{2,1,0:T(8,128)(2,1)} %bitcast.91) | data formatting | bytes 786432 | tf_op jit(solution)/shard_map/convert_element_type | solution.py:106
  158.6 0.5 broadcast.604
  159.1 11.8 %reduce.10 = bf16[2048,96]{1,0:T(8,128)(2,1)S(1)} reduce(bf16[2048,1,96]{2,1,0:T(2,128)(2,1)S(1)} %bitcast.79, bf16[]{:T(256)} %broadcast.604), dimensions={1}, to_apply=%bitcast.69.reduce_sub_computation | reduce | bytes 786434
  170.9 1.6 reshape.481
  172.5 4.6 %all-to-all-start.1 = ((bf16[4,2,24576]{2,1,0:T(2,128)(2,1)}), bf16[4,2,24576]{2,1,0:T(2,128)(2,1)S(1)}, u32[]{:S(2)}, u32[]{:S(2)}) async-start(bf16[4,2,24576]{2,1,0:T(2,128)(2,1)} %reshape.481), calls=%async_computation.2 | async-start | bytes 786432 | tf_op jit(solution)/shard_map/all_to_all | solution.py:105
  177.1 3.5 %fusion.10 = bf16[768,896]{1,0:T(8,128)(2,1)S(1)} fusion(f32[768,896]{1,0:T(8,128)} %get-tuple-element.34, f32[768]{0:T(1024)S(1)} %convert_element_type.65, bf16[768,896]{1,0:T(8,128)(2,1)} %copy-done.3, pred[768]{0:T(1024)(128)(4,1)S(1)} %fusion.25, bf16[768,896]{1,0:T(8,128)(2,1)} %gather_fusion.1), kind=kLoop, calls=%fused_computation.19 | loop fusion | flops 10321920 | bytes 6885120 | tf_op jit(solution)/shard_map/convert_element_type | solution.py:31
  180.6 2.7 %gather_fusion.2 = bf16[512,896]{1,0:T(8,128)(2,1)} fusion(bf16[768,896]{1,0:T(8,128)(2,1)S(1)} %fusion.10, s32[1024]{0:T(1024)S(1)} %pad_clamp_fusion), kind=kCustom, calls=%fused_computation.2 | custom fusion | bytes 1837056 | tf_op jit(solution)/shard_map/gather | solution.py:121
  183.3 12.2 %psum.7 = f32[256]{0:T(256)S(1)} all-reduce(f32[256]{0:T(256)S(1)} %mul.69), channel_id=1, replica_groups=mesh['dp'=8,'expert'=4] {'expert'}, use_global_device_ids=true, to_apply=%region_9.10 | all-reduce | flops 256 | bytes 2048 | tf_op jit(solution)/shard_map/psum | solution.py:117
  195.5 0.6 subtract_multiply_fusion
  196.0 0.8 reshape.482
  196.8 0.6 copy.26
  197.5 0.3 all_to_all.37
  197.8 1.1 convolution_convert_fusion.1
  (44 shorter events, 0.9 us)
Async XLA Ops:
  7.2 48.2 %copy-start = (bf16[1,512,896]{2,1,0:T(8,128)(2,1)S(1)}, bf16[1,512,896]{2,1,0:T(8,128)(2,1)}, u32[]{:S(2)}) copy-start(bf16[1,512,896]{2,1,0:T(8,128)(2,1)} %param.12) | copy-start | bytes 2752516
  7.2 61.9 %all-gather.3.cloned.1.call-start = ((), (), s32[]{:S(2)}) async-start(), calls=%async_computation.4 | async-start | bytes 3538944 | tf_op jit(solution)/shard_map/all_gather | solution.py:83
  15.2 34.2 %copy-start.1 = (s32[4,512]{1,0:T(4,128)S(1)}, s32[4,512]{1,0:T(4,128)}, u32[]{:S(2)}) copy-start(s32[4,512]{1,0:T(4,128)} %param.11) | copy-start | bytes 24580
  34.2 82.4 %all-gather.5.cloned.1.call-start = ((), (), s32[]{:S(2)}) async-start(), calls=%async_computation.6 | async-start | bytes 3538944 | tf_op jit(solution)/shard_map/all_gather | solution.py:92
  49.2 107.1 %reduce-scatter.2.cloned.1.call-start = ((), (), s32[]{:S(2)}) async-start(), calls=%async_computation.5 | async-start | bytes 3538944 | tf_op jit(solution)/shard_map/reduce_scatter | solution.py:98
  55.3 2.8 %copy-start.2 = (bf16[1,512,896]{2,1,0:T(8,128)(2,1)S(1)}, bf16[1,512,896]{2,1,0:T(8,128)(2,1)}, u32[]{:S(2)}) copy-start(bf16[1,512,896]{2,1,0:T(8,128)(2,1)} %param.13) | copy-start | bytes 2752516
  58.2 67.2 %copy-start.3 = (bf16[768,896]{1,0:T(8,128)(2,1)}, bf16[768,896]{1,0:T(8,128)(2,1)S(1)}, u32[]{:S(2)}) copy-start(bf16[768,896]{1,0:T(8,128)(2,1)S(1)} %gather_fusion) | copy-start | bytes 4128772
  58.2 3.5 %copy-start.6 = (u32[32]{0:T(128)S(1)}, u32[32]{0:T(128)}, u32[]{:S(2)}) copy-start(u32[32]{0:T(128)} %constant.137) | copy-start | bytes 388
  69.0 20.9 %copy-start.5 = (f32[1,256]{1,0:T(1,128)S(1)}, f32[1,256]{1,0:T(1,128)}, u32[]{:S(2)}) copy-start(f32[1,256]{1,0:T(1,128)} %param.10) | copy-start | bytes 3076
  116.6 8.8 %copy-start.4 = (bf16[768,896]{1,0:T(8,128)(2,1)S(1)}, bf16[768,896]{1,0:T(8,128)(2,1)}, u32[]{:S(2)}) copy-start(bf16[768,896]{1,0:T(8,128)(2,1)} %gather_fusion.1) | copy-start | bytes 4128772
  116.6 8.8 %copy-start.7 = (bf16[768,2048]{1,0:T(8,128)(2,1)S(1)}, bf16[768,2048]{1,0:T(8,128)(2,1)}, u32[]{:S(2)}) copy-start(bf16[768,2048]{1,0:T(8,128)(2,1)} %all-gather.3.cloned.1.call-done) | copy-start | bytes 9437188
  172.5 23.6 %all-to-all-start.1 = ((bf16[4,2,24576]{2,1,0:T(2,128)(2,1)}), bf16[4,2,24576]{2,1,0:T(2,128)(2,1)S(1)}, u32[]{:S(2)}, u32[]{:S(2)}) async-start(bf16[4,2,24576]{2,1,0:T(2,128)(2,1)} %reshape.481), calls=%async_computation.2 | async-start | bytes 786432 | tf_op jit(solution)/shard_map/all_to_all | solution.py:105
Sparse Core Ops, SparseCore 0:
  34.3 31.2 all-gather.2
  68.1 32.3 all-gather.4
  111.6 44.6 reduce-scatter.1
where the time goes:
time: 206 us; the launch traced here: 205 us
  blocking collectives  68.4 us (33%)
  matrix products  34.2 us (17%)
  other arithmetic  32.7 us (16%)
  waiting for transfers between devices  25.5 us (12%)
  local copies, waits for them, and re-layouts  24.6 us (12%)
  between operations  15.4 us (7%)
  starting transfers between devices  4.72 us (2%)
    reduce_scatter x1, waiting for transfers between devices, local(): lax.psum_scatter(dx_part.astype(jnp.bfloat16), 'dp', scatter_dimension=0,...  25.4 us
    unnamed x2, blocking collectives  24.6 us
    all_to_all x1, blocking collectives, local(): lax.all_to_all(sent_grad, 'expert', split_axis=0, concat_axis=2, tiled=True)  17.8 us
    all_to_all x1, blocking collectives, local(): lax.all_to_all(sent_input, 'expert', split_axis=0, concat_axis=2, tiled=T...  13.8 us
    psum x1, blocking collectives, local(): weighted = lax.psum(router_gate * gate_tokens, 'expert')  12.2 us
    unnamed x1, other arithmetic  11.8 us
    dot_general x1, matrix products, local(): lax.dot_general(up_piece, lax.all_gather(input_rows[0], 'dp', axis=0, til...  8.73 us
    dot_general x1, matrix products, local(): dx_part = jnp.dot(up_grad, upw_block, preferred_element_type=jnp.float32)  8.72 us
  transfers between devices with their start and end apart: 4, of which 1 were waited for; matrix products, arithmetic and copies ran while one was open for 31% of the time, Pallas kernels for 0%

commit v1 on v0

v1 whole, which is shorter than its diff:
```python
import functools

import jax
import jax.numpy as jnp
from jax import lax
from jax.experimental import pallas as pl
from jax.experimental.pallas import tpu as pltpu
from jax.sharding import PartitionSpec as P

LANES = 128
MESH = pl.DeviceIdType.MESH


def bit_orders(shards):
    bits = [1 << k for k in range(shards.bit_length() - 1)]
    return bits, [bits[:1] + bits[1:], bits[:1] + bits[:0:-1]]


def span(bits):
    found = [0]
    for bit in bits:
        found = found + [r | bit for r in found]
    return found


def entry_barrier(experts, bits):
    e = lax.axis_index("expert")
    d = lax.axis_index("dp")
    barrier = pltpu.get_barrier_semaphore()
    for k in range(1, experts):
        pl.semaphore_signal(barrier, inc=1, device_id={"expert": lax.rem(e + k, experts)}, device_id_type=MESH)
    for bit in bits:
        pl.semaphore_signal(barrier, inc=1, device_id={"dp": d ^ bit}, device_id_type=MESH)
    pl.semaphore_wait(barrier, experts - 1 + len(bits))


def dispatch_kernel(experts, shards, g_ref, i_ref, gate_ref, gbuf, ibuf, loc, a2a_s, a2a_r, ag_s, ag_r):
    e = lax.axis_index("expert")
    d = lax.axis_index("dp")
    wd = g_ref.shape[2]
    width = wd * experts
    half = width // 2
    bits, orders = bit_orders(shards)
    entry_barrier(experts, bits)
    kinds = ((g_ref, gbuf), (i_ref, ibuf))

    def cols(src):
        return pl.ds(pl.multiple_of(src * wd, LANES), wd)

    def exchange(kind, k):
        ref, buf = kinds[kind]
        return pltpu.make_async_remote_copy(
            src_ref=ref.at[lax.rem(e + k, experts)],
            dst_ref=buf.at[d, :, cols(e)],
            send_sem=a2a_s.at[kind, k],
            recv_sem=a2a_r.at[kind, k],
            device_id={"expert": lax.rem(e + k, experts)},
            device_id_type=MESH,
        )

    def arrival(kind, k):
        ref, buf = kinds[kind]
        src = lax.rem(e + experts - k, experts)
        return pltpu.make_async_remote_copy(
            src_ref=ref.at[src],
            dst_ref=buf.at[d, :, cols(src)],
            send_sem=a2a_s.at[kind, k],
            recv_sem=a2a_r.at[kind, k],
            device_id={"expert": src},
            device_id_type=MESH,
        )

    for kind in range(2):
        for k in range(1, experts):
            exchange(kind, k).start()
    locals_ = [
        pltpu.make_async_copy(g_ref.at[e], gbuf.at[d, :, cols(e)], loc.at[0]),
        pltpu.make_async_copy(i_ref.at[e], ibuf.at[d, :, cols(e)], loc.at[1]),
        pltpu.make_async_copy(gate_ref, gbuf.at[d, :, pl.ds(width, LANES)], loc.at[2]),
    ]
    for c in locals_:
        c.start()
    streams = []
    for kind in range(2):
        buf = kinds[kind][1]
        ends = (half, buf.shape[2] - half)
        for part in range(2):
            order = orders[part][1:] + orders[part][:1]
            streams.append((buf, pl.ds(part * half, ends[part]), order))

    def piece(n, r, t):
        buf, cut, order = streams[n]
        block = buf.at[d ^ r, :, cut]
        return pltpu.make_async_remote_copy(
            src_ref=block,
            dst_ref=block,
            send_sem=ag_s.at[n, r | order[t]],
            recv_sem=ag_r.at[n, r | order[t]],
            device_id={"dp": d ^ order[t]},
            device_id_type=MESH,
        )

    def landed(n, r):
        buf, cut, order = streams[n]
        block = buf.at[d ^ r, :, cut]
        return pltpu.make_async_remote_copy(
            src_ref=block,
            dst_ref=block,
            send_sem=ag_s.at[n, r],
            recv_sem=ag_r.at[n, r],
            device_id={"dp": d ^ order[0]},
            device_id_type=MESH,
        )

    started = []

    def forward(n, r, first):
        for t in range(first, len(bits)):
            piece(n, r, t).start()
            started.append((n, r, t))

    for kind in range(2):
        locals_[kind].wait()
        if kind == 0:
            locals_[2].wait()
        for k in range(1, experts):
            arrival(kind, k).wait_recv()
        for part in range(2):
            forward(2 * kind + part, 0, 0)
    for t in range(len(bits)):
        for n in range(4):
            order = streams[n][2]
            for r in span(order[:t]):
                got = r | order[t]
                landed(n, got).wait_recv()
                forward(n, got, t + 1)
    for n, r, t in started:
        piece(n, r, t).wait_send()
    for kind in range(2):
        for k in range(1, experts):
            exchange(kind, k).wait_send()


def return_kernel(experts, shards, dx_ref, dots_ref, gate_ref, obuf, own_ref, ra, rb, rd, sbuf, sem_s, sem_r, a2a_s, a2a_r):
    e = lax.axis_index("expert")
    d = lax.axis_index("dp")
    width = dx_ref.shape[2]
    half = width // 2
    wd = width // experts
    bits, orders = bit_orders(shards)
    entry_barrier(experts, bits)
    streams = (
        (dx_ref, pl.ds(0, half), orders[0], ra),
        (dx_ref, pl.ds(half, half), orders[1], rb),
        (dots_ref, pl.ds(0, LANES), orders[0], rd),
    )
    steps = len(bits)

    def slot(n, t, r):
        order = streams[n][2]
        before = sum(1 << (steps - 1 - q) for q in range(t))
        return before + span(order[t + 1 :]).index(r)

    def held(n, t, r):
        src, cut, order, buf = streams[n]
        if t == 0:
            return src.at[d ^ r, :, cut]
        return buf.at[slot(n, t - 1, r)]

    def piece(n, t, r):
        src, cut, order, buf = streams[n]
        place = slot(n, t, r)
        return pltpu.make_async_remote_copy(
            src_ref=held(n, t, r | order[t]),
            dst_ref=buf.at[place],
            send_sem=sem_s.at[n, place],
            recv_sem=sem_r.at[n, place],
            device_id={"dp": d ^ order[t]},
            device_id_type=MESH,
        )

    for r_index in range(1 << (steps - 1)):
        for n in range(3):
            order = streams[n][2]
            r = list(reversed(span(order[1:])))[r_index]
            piece(n, 0, r).start()
    finals = [None] * 3
    for t in range(steps):
        for r_index in range(1 << (steps - 1 - t)):
            for n in range(3):
                src, cut, order, buf = streams[n]
                r = list(reversed(span(order[t + 1 :])))[r_index]
                piece(n, t, r).wait_recv()
                place = slot(n, t, r)
                total = held(n, t, r)[...].astype(jnp.float32) + buf[place].astype(jnp.float32)
                if t == steps - 1:
                    finals[n] = total
                    if n < 2:
                        per = half // wd
                        for q in range(per):
                            sbuf[n * per + q, :, 0:wd] = total[:, q * wd : (q + 1) * wd].astype(jnp.bfloat16)
                else:
                    buf[place] = total.astype(jnp.bfloat16)
                    if r & order[t + 1]:
                        piece(n, t + 1, r ^ order[t + 1]).start()
    dots = finals[2]
    own_ref[...] = dots
    weighted = dots * gate_ref[...]
    high = weighted.astype(jnp.bfloat16)
    low = (weighted - high.astype(jnp.float32)).astype(jnp.bfloat16)
    lane = lax.broadcasted_iota(jnp.int32, high.shape, 1)
    extra = jnp.where(lane == 0, high.astype(jnp.float32), low.astype(jnp.float32)).astype(jnp.bfloat16)
    for q in range(experts):
        sbuf[q, :, wd : wd + LANES] = extra

    def exchange(k):
        to = lax.rem(e + k, experts)
        return pltpu.make_async_remote_copy(
            src_ref=sbuf.at[to],
            dst_ref=obuf.at[e],
            send_sem=a2a_s.at[k],
            recv_sem=a2a_r.at[k],
            device_id={"expert": to},
            device_id_type=MESH,
        )

    def arrival(k):
        src = lax.rem(e + experts - k, experts)
        return pltpu.make_async_remote_copy(
            src_ref=sbuf.at[src],
            dst_ref=obuf.at[src],
            send_sem=a2a_s.at[k],
            recv_sem=a2a_r.at[k],
            device_id={"expert": src},
            device_id_type=MESH,
        )

    for k in range(1, experts):
        exchange(k).start()
    obuf[e] = sbuf[e]
    for k in range(1, experts):
        arrival(k).wait_recv()
    for k in range(1, experts):
        exchange(k).wait_send()
    for n in range(3):
        for t in range(steps):
            for r in span(streams[n][2][t + 1 :]):
                piece(n, t, r).wait_send()


VMEM = pl.BlockSpec(memory_space=pltpu.VMEM)


def dispatch(experts, shards, sent_grad, sent_input, gate_rows):
    _, cap, wd = sent_grad.shape
    width = experts * wd
    return pl.pallas_call(
        functools.partial(dispatch_kernel, experts, shards),
        out_shape=(
            jax.ShapeDtypeStruct((shards, cap, width + LANES), jnp.bfloat16),
            jax.ShapeDtypeStruct((shards, cap, width), jnp.bfloat16),
        ),
        in_specs=[VMEM] * 3,
        out_specs=(VMEM, VMEM),
        scratch_shapes=[
            pltpu.SemaphoreType.DMA((3,)),
            pltpu.SemaphoreType.DMA((2, experts)),
            pltpu.SemaphoreType.DMA((2, experts)),
            pltpu.SemaphoreType.DMA((4, shards)),
            pltpu.SemaphoreType.DMA((4, shards)),
        ],
        compiler_params=pltpu.CompilerParams(collective_id=0, has_side_effects=True),
        name="dispatch",
    )(sent_grad, sent_input, gate_rows)


def give_back(experts, shards, dx, dots, gate_rows):
    _, cap, width = dx.shape
    wd = width // experts
    return pl.pallas_call(
        functools.partial(return_kernel, experts, shards),
        out_shape=(
            jax.ShapeDtypeStruct((experts, cap, wd + LANES), jnp.bfloat16),
            jax.ShapeDtypeStruct((cap, LANES), jnp.float32),
        ),
        in_specs=[VMEM] * 3,
        out_specs=(VMEM, VMEM),
        scratch_shapes=[
            pltpu.VMEM((shards - 1, cap, width // 2), jnp.bfloat16),
            pltpu.VMEM((shards - 1, cap, width // 2), jnp.bfloat16),
            pltpu.VMEM((shards - 1, cap, LANES), jnp.bfloat16),
            pltpu.VMEM((experts, cap, wd + LANES), jnp.bfloat16),
            pltpu.SemaphoreType.DMA((3, shards)),
            pltpu.SemaphoreType.DMA((3, shards)),
            pltpu.SemaphoreType.DMA((experts,)),
            pltpu.SemaphoreType.DMA((experts,)),
        ],
        compiler_params=pltpu.CompilerParams(collective_id=1, has_side_effects=True),
        name="give_back",
    )(dx, dots, gate_rows)


def dot_t(a, b):
    return lax.dot_general(a, b, (((0,), (0,)), ((), ())), preferred_element_type=jnp.float32)


def local(grad_out, saved_inputs, router_probs, chosen, gate_pre, up_pre, w_down, w_up):
    tok_dev, wd = grad_out.shape
    shards = lax.axis_size("dp")
    shard_index = lax.axis_index("dp")
    expert = lax.axis_index("expert")
    experts, slots = chosen.shape
    cap = 3 * slots // (2 * shards)
    width = wd * experts
    bf16 = jnp.bfloat16
    owners = chosen // tok_dev
    firsts = jnp.sum((owners < shard_index).astype(jnp.int32), axis=1)
    slot_iota = jnp.arange(slots, dtype=jnp.int32)
    place = slot_iota[None, :] - firsts[:, None]
    place = jnp.where(owners == shard_index, place, -1)
    hit = place[:, None, :] == jnp.arange(cap, dtype=jnp.int32)[None, :, None]
    local_rows = jnp.max(jnp.where(hit, (chosen - shard_index * tok_dev)[:, None, :], -1), axis=2)
    token_iota = jnp.arange(tok_dev, dtype=jnp.int32)
    picker = (local_rows.reshape(-1)[:, None] == token_iota[None, :]).astype(bf16)
    sent_grad = jnp.dot(picker, grad_out, preferred_element_type=jnp.float32).astype(bf16)
    sent_input = jnp.dot(picker, saved_inputs, preferred_element_type=jnp.float32).astype(bf16)
    own_rows = lax.dynamic_index_in_dim(local_rows, expert, 0, keepdims=False)
    probs = router_probs[0]
    own_hit = own_rows[:, None] == token_iota[None, :]
    gate_own = jnp.sum(jnp.where(own_hit, probs[None, :], 0.0), axis=1)
    gate_wide = jnp.broadcast_to(gate_own[:, None], (cap, LANES))
    gbuf, ibuf = dispatch(
        experts,
        shards,
        sent_grad.reshape(experts, cap, wd),
        sent_input.reshape(experts, cap, wd),
        gate_wide.astype(bf16),
    )
    rows_all = shards * cap
    gbuf = gbuf.reshape(rows_all, width + LANES)
    ibuf = ibuf.reshape(rows_all, width)
    chosen_row = lax.dynamic_index_in_dim(chosen, expert, 0, keepdims=False)
    row_owner = chosen_row // tok_dev
    before = jnp.sum((row_owner[None, :] < row_owner[:, None]).astype(jnp.int32), axis=1)
    slot_place = row_owner * cap + slot_iota - before
    compact = (slot_place[:, None] == jnp.arange(rows_all, dtype=jnp.int32)[None, :]).astype(bf16)
    packed = jnp.dot(compact, gbuf, preferred_element_type=jnp.float32).astype(bf16)
    dout = packed[:, :width]
    gate_slot = packed[:, width:][:, :1]
    gate_value = gate_pre[0].astype(jnp.float32)
    up_value = up_pre[0].astype(jnp.float32)
    sig = jax.nn.sigmoid(gate_value)
    active = gate_value * sig
    hidden = active * up_value
    raw_grad = lax.dot_general(dout, w_down[0], (((1,), (1,)), ((), ())), preferred_element_type=jnp.float32)
    dots = jnp.sum(hidden * raw_grad, axis=1)
    hid_grad = gate_slot.astype(jnp.float32) * raw_grad
    up_grad = (hid_grad * active).astype(bf16)
    gate_grad = (hid_grad * up_value * sig * (1.0 + gate_value * (1.0 - sig))).astype(bf16)
    up_pad = dot_t(compact, up_grad).astype(bf16)
    dx = jnp.dot(up_pad, w_up[0], preferred_element_type=jnp.float32).astype(bf16)
    dots_wide = jnp.broadcast_to(dots.astype(bf16)[:, None], (slots, LANES))
    dots_pad = dot_t(compact, dots_wide).astype(bf16)
    grad_down = dot_t(hidden.astype(bf16), gate_slot * dout).astype(bf16)
    grad_up = dot_t(up_pad, ibuf).astype(bf16)
    spread, dots_own = give_back(
        experts, shards, dx.reshape(shards, cap, width), dots_pad.reshape(shards, cap, LANES), gate_wide
    )
    spread = spread.reshape(experts * cap, wd + LANES)
    summed = dot_t(picker, spread)
    grad_tokens = summed[:, :wd].astype(bf16)
    router_sum = summed[:, wd] + summed[:, wd + 1]
    gate_tokens = jnp.sum(jnp.where(own_hit, dots_own[:, :1], 0.0), axis=0)
    grad_logits = (probs * (gate_tokens - router_sum))[None, :]
    return grad_tokens, grad_logits, grad_down[None], grad_up[None], gate_grad[None]


def solution(mesh):
    in_specs = (
        P("dp", "expert"),
        P("dp", "expert"),
        P("expert", "dp"),
        P(),
        P("expert", None, "dp"),
        P("expert", None, "dp"),
        P("expert", "dp", None),
        P("expert", "dp", None),
    )
    out_specs = (
        P("dp", "expert"),
        P("expert", "dp"),
        P("expert", "dp", None),
        P("expert", "dp", None),
        P("expert", None, "dp"),
    )
    return jax.shard_map(local, mesh=mesh, in_specs=in_specs, out_specs=out_specs, check_vma=False)
```

time: 206 us -> 124 us (0.60)
  Pallas kernels: 0 us -> 85.2 us
  blocking collectives: 68.4 us -> 0 us
  other arithmetic: 32.7 us -> 5.97 us
  waiting for transfers between devices: 25.5 us -> 0 us
  local copies, waits for them, and re-layouts: 24.6 us -> 3.81 us
  between operations: 15.4 us -> 0.78 us
  matrix products: 34.2 us -> 27.4 us
  starting transfers between devices: 4.72 us -> 0 us
    pallas_call x0 -> x2, Pallas kernels: none -> 85.2 us  [the longest x1 47.2 us: dispatch(): pl.pallas_call(functools.partial(dispatch_kernel, experts, shards), out_s...]
    all_to_all x2 -> x0, blocking collectives: 31.6 us -> none  [the longest x1 17.8 us: local(): lax.all_to_all(sent_grad, 'expert', split_axis=0, concat_axis=2, tiled=True)]
    reduce_scatter x1 -> x0, waiting for transfers between devices: 25.4 us -> none  [local(): lax.psum_scatter(dx_part.astype(jnp.bfloat16), 'dp', scatter_dimension=0,...]
    unnamed x2 -> x0, blocking collectives: 24.6 us -> none
    gather x7 -> x0, local copies, waits for them, and re-layouts: 14.9 us -> none  [the longest x3 5.11 us: shard_slots(): picked = jnp.take_along_axis(chosen, places, axis=1)]
    gather x10 -> x0, other arithmetic: 14.7 us -> none  [the longest x3 5.04 us: local(): slot_place = row_owners * capacity + slot_iota - firsts[row_owners]]
    psum x1 -> x0, blocking collectives: 12.2 us -> none  [local(): weighted = lax.psum(router_gate * gate_tokens, 'expert')]
    unnamed x1 -> x0, other arithmetic: 11.8 us -> none
  transfers between devices with their start and end apart: 4 -> 0, of which waited for: 1 -> 0; matrix products, arithmetic and copies ran while one was open for 31% -> 0% of each run, Pallas kernels for 0% -> 0%
where the time goes in v1:
time: 124 us; the launch traced here: 123 us
  Pallas kernels  85.2 us (69%)
  matrix products  27.4 us (22%)
  other arithmetic  5.97 us (5%)
  local copies, waits for them, and re-layouts  3.81 us (3%)
    pallas_call x1, Pallas kernels, dispatch(): pl.pallas_call(functools.partial(dispatch_kernel, experts, shards), out_s...  47.2 us
    pallas_call x1, Pallas kernels, give_back(): pl.pallas_call(functools.partial(return_kernel, experts, shards), out_sha...  38 us
    dot_general x5, matrix products, dot_t(): lax.dot_general(a, b, (((0,), (0,)), ((), ())), preferred_element_type=jn...  13 us
    dot_general x1, matrix products, local(): jnp.dot(up_pad, w_up[0], preferred_element_type=jnp.float32).astype(bf16)  4.79 us
    dot_general x1, matrix products, local(): jnp.dot(compact, gbuf, preferred_element_type=jnp.float32).astype(bf16)  4.19 us

profile of v1, /device:TPU:0, one launch (start us, length us, event | category | flops | bytes accessed | tf_op | source)
XLA Modules:
  0.0 123.2 jit_solution(10971110610184087692)
XLA Ops:
  0.6 0.0 copy-start
  0.7 0.9 convert_reduce_fusion.1
  1.5 0.1 subtract_select_fusion
  1.6 0.2 select_reduce_fusion
  1.8 0.9 select_reduce_fusion.2
  2.7 0.7 broadcast_in_dim.81.gate_ref
  3.4 0.1 eq.67
  3.5 0.0 copy-done
  3.5 1.1 convolution_convert_fusion.3
  4.5 2.0 %convolution_convert_fusion.2 = bf16[384,512]{1,0:T(8,128)(2,1)} fusion(bf16[256,512]{1,0:T(8,128)(2,1)} %param.9, s32[384]{0:T(512)S(1)} %eq.67), kind=kOutput, calls=%fused_computation.29 | convolution fusion | flops 100958208 | bytes 656896 | tf_op jit(solution)/shard_map/dot_general | solution.py:326
  6.5 47.2 %dispatch.1 = (bf16[8,96,2176]{2,1,0:T(8,128)(2,1)}, bf16[8,96,2048]{2,1,0:T(8,128)(2,1)}) custom-call(bf16[4,96,512]{2,1,0:T(8,128)(2,1)} %bitcast.60, bf16[4,96,512]{2,1,0:T(8,128)(2,1)} %bitcast.61, bf16[96,128]{1,0:T(8,128)(2,1)} %broadcast_in_dim.81.gate_ref), custom_call_target="tpu_custom_call" | custom-call | tf_op jit(solution)/shard_map/dispatch/pallas_call | solution.py:257
  53.7 0.7 and_select_fusion
  54.5 0.2 convert_reduce_fusion
  54.7 0.0 copy-start.4
  54.7 4.2 %convolution_convert_fusion = bf16[512,2176]{1,0:T(8,128)(2,1)S(1)} fusion(bf16[768,2176]{1,0:T(8,128)(2,1)} %bitcast.70, s32[512]{0:T(512)S(1)} %add_subtract_fusion), kind=kOutput, calls=%fused_computation | convolution fusion | flops 1712783360 | bytes 5572608 | tf_op jit(solution)/shard_map/dot_general | solution.py:347
  58.9 0.0 copy-done.4
  58.9 0.0 copy-start.1
  59.0 2.4 %fusion.2 = f32[512,896]{1,0:T(8,128)S(1)} fusion(bf16[1,896,2048]{2,1,0:T(8,128)(2,1)S(1)} %copy-done.4, bf16[512,2176]{1,0:T(8,128)(2,1)S(1)} %convolution_convert_fusion), kind=kOutput, calls=%fused_computation.3 | convolution fusion | flops 1879048192 | bytes 7602176 | tf_op jit(solution)/shard_map/dot_general | solution.py:355
  61.3 0.1 slice_reduce_fusion
  61.4 0.0 copy-done.1
  61.5 0.0 copy-start.6
  61.5 1.3 %convolution_convert_fusion.1 = bf16[768,896]{1,0:T(8,128)(2,1)S(1)} fusion(f32[512,896]{1,0:T(8,128)S(1)} %fusion.2, f32[512]{0:T(512)S(1)} %mul.66, s32[512]{0:T(512)S(1)} %add_subtract_fusion, bf16[1,512,896]{2,1,0:T(8,128)(2,1)S(1)} %copy-done.1), kind=kOutput, calls=%fused_computation.25 | convolution fusion | flops 709394432 | bytes 4132864 | tf_op jit(solution)/shard_map/dot_general | solution.py:304
  62.8 0.5 copy-done.6
  63.3 0.0 copy-start.2
  63.3 4.5 %convert_bitcast_fusion = bf16[1,896,2048]{2,1,0:T(8,128)(2,1)} fusion(bf16[768,896]{1,0:T(8,128)(2,1)S(1)} %convolution_convert_fusion.1, bf16[768,2048]{1,0:T(8,128)(2,1)S(1)} %bitcast.71), kind=kOutput, calls=%fused_computation.5 | convolution fusion | flops 2820407296 | bytes 8192000 | tf_op jit(solution)/shard_map/dot_general | solution.py:304
  67.9 0.0 copy-done.2
  67.9 4.2 %convert_bitcast_fusion.1 = bf16[1,896,2048]{2,1,0:T(8,128)(2,1)} fusion(bf16[512,2176]{1,0:T(8,128)(2,1)S(1)} %convolution_convert_fusion, bf16[512]{0:T(512)(128)(2,1)S(1)} %slice_reduce_fusion, bf16[1,512,896]{2,1,0:T(8,128)(2,1)S(1)} %copy-done.2, bf16[1,512,896]{2,1,0:T(8,128)(2,1)S(1)} %copy-done.1), kind=kOutput, calls=%fused_computation.6 | convolution fusion | flops 1885601792 | bytes 7603200 | tf_op jit(solution)/shard_map/dot_general | solution.py:304
  72.0 0.0 copy-start.5
  72.0 2.1 %fusion.24 = (bf16[1,512,896]{2,1,0:T(8,128)(2,1)}, bf16[512]{0:T(512)(128)(2,1)S(1)}) fusion(bf16[1,512,896]{2,1,0:T(8,128)(2,1)S(1)} %copy-done.1, bf16[1,512,896]{2,1,0:T(8,128)(2,1)S(1)} %copy-done.2, f32[512,896]{1,0:T(8,128)S(1)} %fusion.2, f32[512]{0:T(512)S(1)} %mul.66), kind=kLoop, calls=%fused_computation.36 | loop fusion | flops 7798272 | bytes 4590592 | tf_op jit(solution)/shard_map/broadcast_in_dim | solution.py:375
  74.2 1.4 %fusion.19 = bf16[768,128]{1,0:T(8,128)(2,1)} fusion(s32[512]{0:T(512)S(1)} %add_subtract_fusion, bf16[512]{0:T(512)(128)(2,1)S(1)} %get-tuple-element.18), kind=kOutput, calls=%fused_computation.31 | convolution fusion | flops 101154816 | bytes 199680 | tf_op jit(solution)/shard_map/dot_general | solution.py:304
  75.6 0.0 copy-done.5
  75.6 4.8 %fusion.4 = bf16[768,2048]{1,0:T(8,128)(2,1)} fusion(bf16[768,896]{1,0:T(8,128)(2,1)S(1)} %convolution_convert_fusion.1, bf16[1,896,2048]{2,1,0:T(8,128)(2,1)S(1)} %copy-done.5), kind=kOutput, calls=%fused_computation.7 | convolution fusion | flops 2820145152 | bytes 8192000 | tf_op jit(solution)/shard_map/dot_general | solution.py:361
  80.4 0.7 broadcast_in_dim.83.gate_ref
  81.1 0.0 copy-start.3
  81.1 38.0 %give_back.1 = (bf16[4,96,640]{2,1,0:T(8,128)(2,1)}, f32[96,128]{1,0:T(8,128)}) custom-call(bf16[8,96,2048]{2,1,0:T(8,128)(2,1)} %bitcast.59, bf16[8,96,128]{2,1,0:T(8,128)(2,1)} %bitcast.63, f32[96,128]{1,0:T(8,128)} %broadcast_in_dim.83.gate_ref), custom_call_target="tpu_custom_call" | custom-call | tf_op jit(solution)/shard_map/give_back/pallas_call | solution.py:280
  119.1 1.6 %fusion.28 = f32[256,640]{1,0:T(8,128)S(1)} fusion(bf16[384,640]{1,0:T(8,128)(2,1)} %bitcast.62, s32[384]{0:T(512)S(1)} %eq.67), kind=kOutput, calls=%fused_computation.44 | convolution fusion | flops 125927424 | bytes 1148416 | tf_op jit(solution)/shard_map/dot_general | solution.py:304
  120.7 0.2 fusion.32
  120.9 0.9 slice_reduce_fusion.1
  121.8 0.1 select_reduce_fusion.1
  121.9 0.0 copy-done.3
  121.9 0.6 subtract_multiply_fusion
  122.5 0.7 slice.45
  (5 shorter events, 0.0 us)
Async XLA Ops:
  0.6 2.8 %copy-start = (bf16[256,512]{1,0:T(8,128)(2,1)S(1)}, bf16[256,512]{1,0:T(8,128)(2,1)}, u32[]{:S(2)}) copy-start(bf16[256,512]{1,0:T(8,128)(2,1)} %param.8) | copy-start | bytes 786436
  54.7 4.2 %copy-start.4 = (bf16[1,896,2048]{2,1,0:T(8,128)(2,1)S(1)}, bf16[1,896,2048]{2,1,0:T(8,128)(2,1)}, u32[]{:S(2)}) copy-start(bf16[1,896,2048]{2,1,0:T(8,128)(2,1)} %param.14) | copy-start | bytes 11010052
  58.9 2.5 %copy-start.1 = (bf16[1,512,896]{2,1,0:T(8,128)(2,1)S(1)}, bf16[1,512,896]{2,1,0:T(8,128)(2,1)}, u32[]{:S(2)}) copy-start(bf16[1,512,896]{2,1,0:T(8,128)(2,1)} %param.12) | copy-start | bytes 2752516
  61.5 1.9 %copy-start.6 = (bf16[8,96,2048]{2,1,0:T(8,128)(2,1)S(1)}, bf16[8,96,2048]{2,1,0:T(8,128)(2,1)}, u32[]{:S(2)}) copy-start(bf16[8,96,2048]{2,1,0:T(8,128)(2,1)} %get-tuple-element.12) | copy-start | bytes 9437188
  63.3 4.5 %copy-start.2 = (bf16[1,512,896]{2,1,0:T(8,128)(2,1)S(1)}, bf16[1,512,896]{2,1,0:T(8,128)(2,1)}, u32[]{:S(2)}) copy-start(bf16[1,512,896]{2,1,0:T(8,128)(2,1)} %param.13) | copy-start | bytes 2752516
  72.0 3.6 %copy-start.5 = (bf16[1,896,2048]{2,1,0:T(8,128)(2,1)S(1)}, bf16[1,896,2048]{2,1,0:T(8,128)(2,1)}, u32[]{:S(2)}) copy-start(bf16[1,896,2048]{2,1,0:T(8,128)(2,1)} %param.15) | copy-start | bytes 11010052
  81.1 40.8 %copy-start.3 = (f32[1,256]{1,0:T(1,128)S(1)}, f32[1,256]{1,0:T(1,128)}, u32[]{:S(2)}) copy-start(f32[1,256]{1,0:T(1,128)} %param.10) | copy-start | bytes 3076

commit v2 on v1

--- a/solution.py
+++ b/solution.py
@@ -34,7 +34,9 @@
     pl.semaphore_wait(barrier, experts - 1 + len(bits))
 
 
-def dispatch_kernel(experts, shards, g_ref, i_ref, gate_ref, gbuf, ibuf, loc, a2a_s, a2a_r, ag_s, ag_r):
+def dispatch_kernel(
+    experts, shards, g_ref, i_ref, gate_ref, compact_ref, w_ref, ibuf, packed, raw, gbuf, wbuf, loc, a2a_s, a2a_r, ag_s, ag_r
+):
     e = lax.axis_index("expert")
     d = lax.axis_index("dp")
     wd = g_ref.shape[2]
@@ -80,6 +82,8 @@
     ]
     for c in locals_:
         c.start()
+    weights = pltpu.make_async_copy(w_ref, wbuf, loc.at[3])
+    weights.start()
     streams = []
     for kind in range(2):
         buf = kinds[kind][1]
@@ -119,21 +123,52 @@
             piece(n, r, t).start()
             started.append((n, r, t))
 
-    for kind in range(2):
+    def begin(kind):
         locals_[kind].wait()
-        if kind == 0:
-            locals_[2].wait()
         for k in range(1, experts):
             arrival(kind, k).wait_recv()
         for part in range(2):
             forward(2 * kind + part, 0, 0)
-    for t in range(len(bits)):
-        for n in range(4):
+
+    def receive(t, chosen_streams):
+        for n in chosen_streams:
             order = streams[n][2]
             for r in span(order[:t]):
                 got = r | order[t]
                 landed(n, got).wait_recv()
                 forward(n, got, t + 1)
+
+    rows = compact_ref.shape[1] // 2
+
+    def pack(tile, carry):
+        cut = pl.ds(pl.multiple_of(tile * rows, rows), rows)
+        total = jnp.dot(compact_ref[0, cut, :], gbuf[0], preferred_element_type=jnp.float32)
+        for q in range(1, shards):
+            total += jnp.dot(compact_ref[q, cut, :], gbuf[q], preferred_element_type=jnp.float32)
+        packed[cut, :] = total.astype(jnp.bfloat16)
+        return carry
+
+    def multiply(tile, carry):
+        cut = pl.ds(pl.multiple_of(tile * rows, rows), rows)
+        raw[cut, :] = lax.dot_general(
+            packed[cut, 0:width], wbuf[...], (((1,), (1,)), ((), ())), preferred_element_type=jnp.float32
+        )
+        return carry
+
+    locals_[2].wait()
+    begin(0)
+    receive(0, (0, 1))
+    begin(1)
+    for t in range(1, len(bits) - 1):
+        receive(t, (0, 1))
+    receive(0, (2, 3))
+    receive(len(bits) - 1, (0, 1))
+    lax.fori_loop(0, 2, pack, 0)
+    for t in range(1, len(bits) - 1):
+        receive(t, (2, 3))
+    weights.wait()
+    lax.fori_loop(0, 2, multiply, 0)
+    receive(len(bits) - 1, (2, 3))
     for n, r, t in started:
         piece(n, r, t).wait_send()
     for kind in range(2):
@@ -251,19 +286,22 @@
 VMEM = pl.BlockSpec(memory_space=pltpu.VMEM)
 
 
-def dispatch(experts, shards, sent_grad, sent_input, gate_rows):
+def dispatch(experts, shards, sent_grad, sent_input, gate_rows, compact, weights):
     _, cap, wd = sent_grad.shape
     width = experts * wd
     return pl.pallas_call(
         functools.partial(dispatch_kernel, experts, shards),
         out_shape=(
-            jax.ShapeDtypeStruct((shards, cap, width + LANES), jnp.bfloat16),
             jax.ShapeDtypeStruct((shards, cap, width), jnp.bfloat16),
+            jax.ShapeDtypeStruct((compact.shape[1], width + LANES), jnp.bfloat16),
+            jax.ShapeDtypeStruct((compact.shape[1], weights.shape[0]), jnp.float32),
         ),
-        in_specs=[VMEM] * 3,
-        out_specs=(VMEM, VMEM),
+        in_specs=[VMEM] * 4 + [pl.BlockSpec(memory_space=pl.ANY)],
+        out_specs=(VMEM, VMEM, VMEM),
         scratch_shapes=[
-            pltpu.SemaphoreType.DMA((3,)),
+            pltpu.VMEM((shards, cap, width + LANES), jnp.bfloat16),
+            pltpu.VMEM(weights.shape, jnp.bfloat16),
+            pltpu.SemaphoreType.DMA((4,)),
             pltpu.SemaphoreType.DMA((2, experts)),
             pltpu.SemaphoreType.DMA((2, experts)),
             pltpu.SemaphoreType.DMA((4, shards)),
@@ -271,7 +309,7 @@
         ],
         compiler_params=pltpu.CompilerParams(collective_id=0, has_side_effects=True),
         name="dispatch",
-    )(sent_grad, sent_input, gate_rows)
+    )(sent_grad, sent_input, gate_rows, compact, weights)
 
 
 def give_back(experts, shards, dx, dots, gate_rows):
@@ -329,22 +367,24 @@
     own_hit = own_rows[:, None] == token_iota[None, :]
     gate_own = jnp.sum(jnp.where(own_hit, probs[None, :], 0.0), axis=1)
     gate_wide = jnp.broadcast_to(gate_own[:, None], (cap, LANES))
-    gbuf, ibuf = dispatch(
+    rows_all = shards * cap
+    chosen_row = lax.dynamic_index_in_dim(chosen, expert, 0, keepdims=False)
+    row_owner = chosen_row // tok_dev
+    before = jnp.sum((row_owner[None, :] < row_owner[:, None]).astype(jnp.int32), axis=1)
+    slot_place = row_owner * cap + slot_iota - before
+    compact = (slot_place[:, None] == jnp.arange(rows_all, dtype=jnp.int32)[None, :]).astype(bf16)
+    padded = jnp.arange(rows_all, dtype=jnp.int32).reshape(shards, 1, cap)
+    blocks = (slot_place[None, :, None] == padded).astype(bf16)
+    ibuf, packed, raw_grad = dispatch(
         experts,
         shards,
         sent_grad.reshape(experts, cap, wd),
         sent_input.reshape(experts, cap, wd),
         gate_wide.astype(bf16),
+        blocks,
+        w_down[0],
     )
-    rows_all = shards * cap
-    gbuf = gbuf.reshape(rows_all, width + LANES)
     ibuf = ibuf.reshape(rows_all, width)
-    chosen_row = lax.dynamic_index_in_dim(chosen, expert, 0, keepdims=False)
-    row_owner = chosen_row // tok_dev
-    before = jnp.sum((row_owner[None, :] < row_owner[:, None]).astype(jnp.int32), axis=1)
-    slot_place = row_owner * cap + slot_iota - before
-    compact = (slot_place[:, None] == jnp.arange(rows_all, dtype=jnp.int32)[None, :]).astype(bf16)
-    packed = jnp.dot(compact, gbuf, preferred_element_type=jnp.float32).astype(bf16)
     dout = packed[:, :width]
     gate_slot = packed[:, width:][:, :1]
     gate_value = gate_pre[0].astype(jnp.float32)
@@ -352,7 +392,6 @@
     sig = jax.nn.sigmoid(gate_value)
     active = gate_value * sig
     hidden = active * up_value
-    raw_grad = lax.dot_general(dout, w_down[0], (((1,), (1,)), ((), ())), preferred_element_type=jnp.float32)
     dots = jnp.sum(hidden * raw_grad, axis=1)
     hid_grad = gate_slot.astype(jnp.float32) * raw_grad
     up_grad = (hid_grad * active).astype(bf16)

time: 124 us -> 122 us (0.984)
  matrix products: 27.4 us -> 21.5 us
  Pallas kernels: 85.2 us -> 88.3 us
    dot_general x2 -> x0, matrix products: 6.55 us -> none  [the longest x1 4.19 us: local(): jnp.dot(compact, gbuf, preferred_element_type=jnp.float32).astype(bf16)]
    pallas_call x1, Pallas kernels: 47.2 us -> 51.1 us  [dispatch(): pl.pallas_call(functools.partial(dispatch_kernel, experts, shards), out_s...]
    dot_general x5, matrix products: 13 us -> 14.6 us  [dot_t(): lax.dot_general(a, b, (((0,), (0,)), ((), ())), preferred_element_type=jn...]
    convert_element_type x0 -> x1, other arithmetic: none -> 1.24 us  [local(): blocks = (slot_place[None, :, None] == padded).astype(bf16)]
where the time goes in v2:
time: 122 us
  Pallas kernels  88.3 us (72%)
  matrix products  21.5 us (18%)
  other arithmetic  7.17 us (6%)
  local copies, waits for them, and re-layouts  4.18 us (3%)
    pallas_call x1, Pallas kernels, dispatch(): pl.pallas_call(functools.partial(dispatch_kernel, experts, shards), out_s...  51.1 us
    pallas_call x1, Pallas kernels, give_back(): pl.pallas_call(functools.partial(return_kernel, experts, shards), out_sha...  37.2 us
    dot_general x5, matrix products, dot_t(): lax.dot_general(a, b, (((0,), (0,)), ((), ())), preferred_element_type=jn...  14.6 us
    dot_general x1, matrix products, local(): jnp.dot(up_pad, w_up[0], preferred_element_type=jnp.float32).astype(bf16)  4.79 us

profile of v2, /device:TPU:0, one launch (start us, length us, event | category | flops | bytes accessed | tf_op | source)
XLA Modules:
  0.0 122.0 jit_solution(16480269063133586968)
XLA Ops:
  0.6 0.0 copy-start
  0.6 0.0 copy-start.4
  0.7 0.9 convert_reduce_fusion.1
  1.5 0.1 subtract_select_fusion
  1.6 0.2 select_reduce_fusion
  1.8 0.9 select_reduce_fusion.2
  2.7 0.7 broadcast_in_dim.82.gate_ref
  3.4 0.7 and_select_fusion
  4.1 0.2 convert_reduce_fusion
  4.4 1.2 %compare_convert_fusion.compact_ref = bf16[8,512,96]{2,1,0:T(8,128)(2,1)} fusion(s32[8,96]{1,0:T(8,128)S(1)} %multiply_add_fusion, s32[512]{0:T(512)S(1)} %add_subtract_fusion), kind=kLoop, calls=%fused_computation.12 | loop fusion | flops 786432 | bytes 791552 | tf_op jit(solution)/shard_map/convert_element_type | solution.py:377
  5.6 0.1 eq.80
  5.7 0.0 copy-done
  5.7 1.1 convolution_convert_fusion.2
  6.8 0.0 copy-done.4
  6.8 1.1 convolution_convert_fusion.1
  7.9 0.0 copy-start.2
  7.9 51.1 %dispatch.1 = (bf16[8,96,2048]{2,1,0:T(8,128)(2,1)}, bf16[512,2176]{1,0:T(8,128)(2,1)}, f32[512,896]{1,0:T(8,128)}) custom-call(bf16[4,96,512]{2,1,0:T(8,128)(2,1)} %bitcast.57, bf16[4,96,512]{2,1,0:T(8,128)(2,1)} %bitcast.58, bf16[96,128]{1,0:T(8,128)(2,1)} %broadcast_in_dim.82.gate_ref, bf16[8,512,96]{2,1,0:T(8,128)(2,1)} %compare_convert_fusion.compact_ref, ...), custom_call_target="tpu_custom_call" | custom-call | tf_op jit(solution)/shard_map/dispatch/pallas_call | solution.py:292
  59.0 1.0 slice_reduce_fusion
  60.0 0.0 copy-done.2
  60.0 0.0 copy-start.8
  60.0 2.9 %convolution_convert_fusion = bf16[768,896]{1,0:T(8,128)(2,1)S(1)} fusion(f32[512,896]{1,0:T(8,128)} %get-tuple-element.11, f32[512]{0:T(512)S(1)} %mul.70, s32[512]{0:T(512)S(1)} %add_subtract_fusion, bf16[1,512,896]{2,1,0:T(8,128)(2,1)S(1)} %copy-done.2), kind=kOutput, calls=%fused_computation.22 | convolution fusion | flops 709394432 | bytes 4132864 | tf_op jit(solution)/shard_map/dot_general | solution.py:342
  62.9 0.0 copy-done.8
  63.0 0.0 copy-start.3
  63.0 0.0 copy-start.5
  63.0 4.5 %convert_bitcast_fusion = bf16[1,896,2048]{2,1,0:T(8,128)(2,1)} fusion(bf16[768,896]{1,0:T(8,128)(2,1)S(1)} %convolution_convert_fusion, bf16[768,2048]{1,0:T(8,128)(2,1)S(1)} %bitcast.67), kind=kOutput, calls=%fused_computation.2 | convolution fusion | flops 2820407296 | bytes 8192000 | tf_op jit(solution)/shard_map/dot_general | solution.py:342
  67.5 0.0 copy-done.3
  67.5 0.0 copy-done.5
  67.5 0.0 copy-start.1
  67.5 4.1 %convert_bitcast_fusion.1 = bf16[1,896,2048]{2,1,0:T(8,128)(2,1)} fusion(bf16[512,2176]{1,0:T(8,128)(2,1)S(1)} %copy-done.5, bf16[512]{0:T(512)(128)(2,1)S(1)} %slice_reduce_fusion, bf16[1,512,896]{2,1,0:T(8,128)(2,1)S(1)} %copy-done.3, bf16[1,512,896]{2,1,0:T(8,128)(2,1)S(1)} %copy-done.2), kind=kOutput, calls=%fused_computation.3 | convolution fusion | flops 1885601792 | bytes 7603200 | tf_op jit(solution)/shard_map/dot_general | solution.py:342
  71.7 0.0 copy-done.1
  71.7 0.0 copy-start.7
  71.7 2.1 %fusion.21 = (bf16[1,512,896]{2,1,0:T(8,128)(2,1)}, bf16[512]{0:T(512)(128)(2,1)S(1)}) fusion(bf16[1,512,896]{2,1,0:T(8,128)(2,1)S(1)} %copy-done.2, bf16[1,512,896]{2,1,0:T(8,128)(2,1)S(1)} %copy-done.3, f32[512,896]{1,0:T(8,128)S(1)} %copy-done.1, f32[512]{0:T(512)S(1)} %mul.70), kind=kLoop, calls=%fused_computation.33 | loop fusion | flops 7798272 | bytes 4590592 | tf_op jit(solution)/shard_map/broadcast_in_dim | solution.py:414
  73.7 1.4 %fusion.16 = bf16[768,128]{1,0:T(8,128)(2,1)} fusion(s32[512]{0:T(512)S(1)} %add_subtract_fusion, bf16[512]{0:T(512)(128)(2,1)S(1)} %get-tuple-element.20), kind=kOutput, calls=%fused_computation.28 | convolution fusion | flops 101154816 | bytes 199680 | tf_op jit(solution)/shard_map/dot_general | solution.py:342
  75.2 0.0 copy-done.7
  75.2 4.8 %fusion.2 = bf16[768,2048]{1,0:T(8,128)(2,1)} fusion(bf16[768,896]{1,0:T(8,128)(2,1)S(1)} %convolution_convert_fusion, bf16[1,896,2048]{2,1,0:T(8,128)(2,1)S(1)} %copy-done.7), kind=kOutput, calls=%fused_computation.4 | convolution fusion | flops 2820145152 | bytes 8192000 | tf_op jit(solution)/shard_map/dot_general | solution.py:400
  80.0 0.7 broadcast_in_dim.84.gate_ref
  80.6 0.0 copy-start.6
  80.7 37.2 %give_back.1 = (bf16[4,96,640]{2,1,0:T(8,128)(2,1)}, f32[96,128]{1,0:T(8,128)}) custom-call(bf16[8,96,2048]{2,1,0:T(8,128)(2,1)} %bitcast.56, bf16[8,96,128]{2,1,0:T(8,128)(2,1)} %bitcast.60, f32[96,128]{1,0:T(8,128)} %broadcast_in_dim.84.gate_ref), custom_call_target="tpu_custom_call" | custom-call | tf_op jit(solution)/shard_map/give_back/pallas_call | solution.py:318
  117.9 1.6 %fusion.24 = f32[256,640]{1,0:T(8,128)S(1)} fusion(bf16[384,640]{1,0:T(8,128)(2,1)} %bitcast.59, s32[384]{0:T(512)S(1)} %eq.80), kind=kOutput, calls=%fused_computation.40 | convolution fusion | flops 125927424 | bytes 1148416 | tf_op jit(solution)/shard_map/dot_general | solution.py:342
  119.5 0.2 fusion.28
  119.7 0.9 slice_reduce_fusion.1
  120.6 0.1 select_reduce_fusion.1
  120.7 0.0 copy-done.6
  120.7 0.6 subtract_multiply_fusion
  121.3 0.7 slice.41
  (6 shorter events, 0.0 us)
Async XLA Ops:
  0.6 5.1 %copy-start = (bf16[256,512]{1,0:T(8,128)(2,1)S(1)}, bf16[256,512]{1,0:T(8,128)(2,1)}, u32[]{:S(2)}) copy-start(bf16[256,512]{1,0:T(8,128)(2,1)} %param.8) | copy-start | bytes 786436
  0.6 6.2 %copy-start.4 = (bf16[256,512]{1,0:T(8,128)(2,1)S(1)}, bf16[256,512]{1,0:T(8,128)(2,1)}, u32[]{:S(2)}) copy-start(bf16[256,512]{1,0:T(8,128)(2,1)} %param.9) | copy-start | bytes 786436
  7.9 52.1 %copy-start.2 = (bf16[1,512,896]{2,1,0:T(8,128)(2,1)S(1)}, bf16[1,512,896]{2,1,0:T(8,128)(2,1)}, u32[]{:S(2)}) copy-start(bf16[1,512,896]{2,1,0:T(8,128)(2,1)} %param.12) | copy-start | bytes 2752516
  60.0 2.9 %copy-start.8 = (bf16[8,96,2048]{2,1,0:T(8,128)(2,1)S(1)}, bf16[8,96,2048]{2,1,0:T(8,128)(2,1)}, u32[]{:S(2)}) copy-start(bf16[8,96,2048]{2,1,0:T(8,128)(2,1)} %get-tuple-element.14) | copy-start | bytes 9437188
  63.0 4.6 %copy-start.3 = (bf16[1,512,896]{2,1,0:T(8,128)(2,1)S(1)}, bf16[1,512,896]{2,1,0:T(8,128)(2,1)}, u32[]{:S(2)}) copy-start(bf16[1,512,896]{2,1,0:T(8,128)(2,1)} %param.13) | copy-start | bytes 2752516
  63.0 4.5 %copy-start.5 = (bf16[512,2176]{1,0:T(8,128)(2,1)S(1)}, bf16[512,2176]{1,0:T(8,128)(2,1)}, u32[]{:S(2)}) copy-start(bf16[512,2176]{1,0:T(8,128)(2,1)} %get-tuple-element.10) | copy-start | bytes 6684676
  67.5 4.1 %copy-start.1 = (f32[512,896]{1,0:T(8,128)S(1)}, f32[512,896]{1,0:T(8,128)}, u32[]{:S(2)}) copy-start(f32[512,896]{1,0:T(8,128)} %get-tuple-element.11) | copy-start | bytes 5505028
  71.7 3.5 %copy-start.7 = (bf16[1,896,2048]{2,1,0:T(8,128)(2,1)S(1)}, bf16[1,896,2048]{2,1,0:T(8,128)(2,1)}, u32[]{:S(2)}) copy-start(bf16[1,896,2048]{2,1,0:T(8,128)(2,1)} %param.15) | copy-start | bytes 11010052
  80.6 40.0 %copy-start.6 = (f32[1,256]{1,0:T(1,128)S(1)}, f32[1,256]{1,0:T(1,128)}, u32[]{:S(2)}) copy-start(f32[1,256]{1,0:T(1,128)} %param.10) | copy-start | bytes 3076
